TPU v7x, 32 devices: a whole 2x2x4 slice. The times are simulated.
32 devices in a mesh: lat: 8 (over z, y), lon: 4 (over x, core).
Axes of the slice: x: 2, y: 2, z: 4, core: 2. Of those that a mesh axis runs over, the one named last changes fastest.
Arguments:
- raw_fields: bfloat16 [32, 160, 1440], P(('lat', 'lon')), may hold values from -6 to 6
- embed_weight: bfloat16 [32, 4, 4, 1024], replicated, may hold values from -0.25 to 0.25
- embed_bias: float32 [1024], replicated, may hold values from -3 to 3
- conv_weight: bfloat16 [3, 3, 1024, 1024], replicated, may hold values from -0.0625 to 0.0625
- conv_bias: float32 [1024], replicated, may hold values from -3 to 3
Outputs:
- features: bfloat16 [40, 360, 1024], P('lat', 'lon')
All inputs are finite; a program needn't handle non-finite values.
Results may differ from a plain program's by a relative error of at most 0.0049.
Values may be sent and summed in bfloat16 or wider, within the bound.
A program may use at most 192 MiB of HBM per device.

v0:
```python
import functools

import jax
import jax.numpy as jnp
from jax import lax
from jax.experimental import pallas as pl
from jax.experimental.pallas import tpu as pltpu
from jax.sharding import PartitionSpec as P

PATCH = 4
LANES = 128
CELLS = PATCH * PATCH
MESH = pl.DeviceIdType.MESH


def kernel(
    dims,
    raw_hbm, ew_hbm, eb_hbm, cw_hbm, cb_hbm,
    out_ref,
    eb_ref, cb_ref, raw, sides, send, send_far, recv, recv_far, near, ew_raw, ew, cw, comb, bias, taps,
    eb_sem, cb_sem, raw_sem, ew_sem, cw_sem, send_sem, recv_sem, fsend_sem, frecv_sem, nsend_sem, nrecv_sem,
):
    lat_n, lon_n, height, breadth, rows, cols, width = dims
    total = lat_n * lon_n
    lat = lax.axis_index("lat")
    lon = lax.axis_index("lon")
    me = lat * lon_n + lon
    row_slots = taps.shape[0] // (rows + 2)
    composed = total * CELLS <= width
    tap_width = total * CELLS if composed else width
    spare = LANES - row_slots

    raw_copy = pltpu.make_async_copy(raw_hbm.at[0], raw, raw_sem)
    raw_copy.start()

    def peer(step):
        k = step // lon_n
        r = step % lon_n
        off = lat_n // 2 + (2 * (k % 2) - 1) * ((k + 1) // 2)
        return (lat + off + lat_n) % lat_n, (lon + r + 1) % lon_n

    barrier = pltpu.get_barrier_semaphore()

    @pl.loop(0, total - 1, unroll=total <= 32)
    def _(step):
        a, b = peer(step)
        pl.semaphore_signal(barrier, inc=1, device_id=(a, b), device_id_type=MESH)

    ew_copy = pltpu.make_async_copy(ew_hbm, ew_raw, ew_sem)
    ew_copy.start()
    bias_copies = [
        pltpu.make_async_copy(eb_hbm, eb_ref, eb_sem),
        pltpu.make_async_copy(cb_hbm, cb_ref, cb_sem),
    ]
    for copy in bias_copies:
        copy.start()
    cw_copies = []
    for p in range(3):
        for q in range(3):
            copy = pltpu.make_async_copy(cw_hbm.at[p, q], cw.at[p, q], cw_sem.at[3 * p + q])
            copy.start()
            cw_copies.append(copy)

    patches = breadth // PATCH
    group = min(lat_n, 8)
    group_rows = group * rows * PATCH
    block = group * CELLS
    lane = lax.broadcasted_iota(jnp.int32, (1, PATCH * LANES), 1)
    slot = lane % LANES
    cell = lane // LANES
    m = lax.broadcasted_iota(jnp.int32, (rows * block, 1), 0)
    target = (
        (m % PATCH) * group_rows
        + ((m // CELLS) % group) * (rows * PATCH)
        + (m // block) * PATCH
        + (m // PATCH) % PATCH
    )
    c = lax.broadcasted_iota(jnp.int32, (rows * block, PATCH * group_rows), 1)
    pick_rows = jnp.where(c == target, 1.0, 0.0).astype(jnp.bfloat16)
    pickers = []
    for l in range(lon_n):
        wanted = [PATCH * ((cols * l - 1 + s) % patches) for s in range(cols + 2)]
        used = sorted({x // LANES for w in wanted for x in (w, w + PATCH - 1)})
        patch = (cols * l - 1 + slot + patches) % patches
        column = jnp.where(slot < cols + 2, PATCH * patch + cell, -1)
        picks = []
        for b in used:
            k = lax.broadcasted_iota(jnp.int32, (LANES, PATCH * LANES), 0) + b * LANES
            picks.append(jnp.where(k == column, 1.0, 0.0).astype(jnp.bfloat16))
        pickers.append((used, jnp.concatenate(picks, axis=0)))
    raw_copy.wait()
    for g in range(lat_n // group):
        for l in range(lon_n):
            used, picks = pickers[l]
            parts = []
            for b in used:
                part = raw[
                    g * group_rows : (g + 1) * group_rows,
                    b * LANES : min((b + 1) * LANES, breadth),
                ]
                short = LANES - part.shape[1]
                if short:
                    fill = jnp.zeros((group_rows, short), jnp.bfloat16)
                    part = jnp.concatenate([part, fill], axis=1)
                parts.append(part)
            found = jnp.dot(
                jnp.concatenate(parts, axis=1), picks, preferred_element_type=jnp.float32
            ).astype(jnp.bfloat16)
            for j in range(PATCH):
                sides[j * group_rows : (j + 1) * group_rows, l * LANES : (l + 1) * LANES] = (
                    found[:, j * LANES : (j + 1) * LANES]
                )
        tiles = jnp.dot(pick_rows, sides[...], preferred_element_type=jnp.float32)
        low = lax.broadcasted_iota(jnp.int32, (block, LANES), 1) < row_slots
        for l in range(lon_n):
            column = tiles[:, l * LANES : (l + 1) * LANES]
            per_row = [column[a * block : (a + 1) * block] for a in range(rows)]
            spread = per_row[rows - 2]
            for k in range(rows - 1):
                moved = spread if k * spare >= row_slots else pltpu.roll(
                    spread, row_slots - k * spare, 1
                )
                kept = per_row[k if k < rows - 2 else rows - 1]
                packed = jnp.where(low, kept, moved).astype(jnp.bfloat16)
                send[g * group : (g + 1) * group, l, :, k * LANES : (k + 1) * LANES] = (
                    packed.reshape(group, CELLS, LANES)
                )
            first = per_row[0].astype(jnp.bfloat16).reshape(group, CELLS, LANES)
            final = per_row[rows - 1].astype(jnp.bfloat16).reshape(group, CELLS, LANES)
            for t in range(group):
                to = g * group + (t + 1 if t % 2 else t - 1)
                if 0 <= to < lat_n:
                    send_far[to, l] = final[t] if t % 2 else first[t]
            for t in (0, lat_n - 1):
                if t // group == g:
                    send_far[t, l] = jnp.zeros((CELLS, LANES), jnp.bfloat16)

    early = 0
    ew_copy.wait()
    for copy in bias_copies:
        copy.wait()
    for i in range(PATCH):
        ew[:total, PATCH * i : PATCH * (i + 1), :] = ew_raw[:, i]
    if composed:
        high = eb_ref[...].astype(jnp.bfloat16)
        rest = eb_ref[...] - high.astype(jnp.float32)
        index = lax.broadcasted_iota(jnp.int32, (CELLS, width), 0)
        both = jnp.where(index == 0, high.astype(jnp.float32), jnp.where(index == 1, rest, 0.0))
        ew[total] = both.astype(jnp.bfloat16)

        def compose(start, stop):
            @pl.loop(start, stop)
            def _(tap):
                p, q = tap // 3, tap % 3
                pltpu.make_async_copy(cw_hbm.at[p, q], cw.at[p, q], cw_sem.at[tap]).wait()
                left = ew[...].reshape((total + 1) * CELLS, width)
                for n in range(0, width, 256):
                    product = jnp.dot(
                        left, cw[p, q, :, n : n + 256], preferred_element_type=jnp.float32
                    )
                    comb[p, q, :, n : n + 256] = product[:tap_width].astype(jnp.bfloat16)
                    bias[tap, :, n : n + 256] = product[tap_width : tap_width + 8]

        compose(0, early)

    pl.semaphore_wait(barrier, total - 1)

    def exchange(source, dest, out_sem, in_sem):
        @pl.loop(0, total - 1, unroll=total <= 32)
        def _(step):
            a, b = peer(step)
            pltpu.make_async_remote_copy(
                src_ref=source.at[a, b],
                dst_ref=dest.at[me],
                send_sem=out_sem,
                recv_sem=in_sem,
                device_id=(a, b),
                device_id_type=MESH,
            ).start()

        pltpu.make_async_copy(source.at[lat, lon], dest.at[me], in_sem).start()

    exchange(send, recv, send_sem, recv_sem)

    if composed:
        compose(early, 9)

    pltpu.make_async_copy(recv, recv, recv_sem).wait()
    odd = lat % 2
    edge_tile = pl.multiple_of((rows - 2) * LANES * (1 - odd), LANES)
    pair_copy = pltpu.make_async_remote_copy(
        src_ref=recv.at[:, :, pl.ds(edge_tile, LANES)],
        dst_ref=near,
        send_sem=nsend_sem,
        recv_sem=nrecv_sem,
        device_id=(lat + 1 - 2 * odd, lon),
        device_id_type=MESH,
    )
    pair_copy.start()
    exchange(send_far, recv_far, fsend_sem, frecv_sem)

    def place(row, n, tokens):
        lanes = slice(n, n + tokens.shape[1])
        start = row * row_slots
        if not isinstance(start, int):
            start = pl.multiple_of(start, 16)
        for q in range(3):
            shifted = tokens if q == 0 else pltpu.roll(tokens, row_slots - q, 0)
            taps[pl.ds(start, row_slots), q * tap_width + lanes.start : q * tap_width + lanes.stop] = (
                shifted.astype(jnp.bfloat16)
            )

    step_n = 256
    kernel_weights = comb if composed else cw

    def embed(x, n):
        weights = ew[:total, :, n : n + step_n].reshape(total * CELLS, step_n)
        return jnp.dot(x, weights, preferred_element_type=jnp.float32) + eb_ref[:, n : n + step_n]

    x = recv[...].reshape(total * CELLS, recv.shape[2]).T
    for n in range(0, tap_width, step_n):
        e = x[:, n : n + step_n].astype(jnp.float32) if composed else embed(x, n)
        chunks = []
        for k in range(rows - 1):
            row = k if k < rows - 2 else rows - 1
            place(row + 1, n, e[k * LANES : k * LANES + row_slots])
            if k * spare < row_slots:
                chunks.append(e[k * LANES + row_slots : (k + 1) * LANES])
        place(rows - 1, n, jnp.concatenate(chunks, axis=0)[:row_slots])

    top = jnp.where(lat > 0, 1.0, 0.0)
    bottom = jnp.where(lat < lat_n - 1, 1.0, 0.0)
    if not composed:
        for copy in cw_copies:
            copy.wait()

    def row_bias(a, n, scales):
        total_bias = cb_ref[:, pl.ds(n, step_n)]
        if composed:
            for p in range(3):
                part = 0.0
                for q in range(3):
                    part += bias[3 * p + q, 0:1, pl.ds(n, step_n)] + bias[3 * p + q, 1:2, pl.ds(n, step_n)]
                if scales is not None:
                    part *= scales[p]
                total_bias = total_bias + part
        return total_bias

    def tap_rows(row, count):
        if isinstance(row, int):
            return taps[row * row_slots : (row + count) * row_slots, :]
        return taps[pl.ds(pl.multiple_of(row * row_slots, 16), count * row_slots), :]

    def conv(a, count, scales):
        @pl.loop(0, width // (2 * step_n))
        def _(block_n):
            for half in range(2):
                n = pl.multiple_of(block_n * (2 * step_n) + half * step_n, step_n)
                summed = None
                for p in range(3):
                    left = tap_rows(a + p, count)
                    weights = kernel_weights[p, :, :, pl.ds(n, step_n)]
                    weights = weights.reshape(3 * tap_width, step_n)
                    part = jnp.dot(left, weights, preferred_element_type=jnp.float32)
                    summed = part if summed is None else summed + part
                shift = row_bias(a, n, scales)
                for k in range(count):
                    value = summed[k * row_slots : (k + 1) * row_slots] + shift
                    value = 0.5 * value * (1.0 + lax.erf(value * (0.5 ** 0.5)))
                    out_ref[a + k, :, pl.ds(n, step_n)] = value[:cols].astype(jnp.bfloat16)

    conv(1, rows - 2, None)

    inside = top * bottom
    even = jnp.where(odd > 0, 0.0, 1.0)
    scales = (1.0 - even * (1.0 - inside), 1.0, 1.0 - (1.0 - even) * (1.0 - inside))

    def edge(source, below, factor, row_scales):
        x = source[...].reshape(total * CELLS, LANES).T[:row_slots]
        for n in range(0, tap_width, step_n):
            if composed:
                e = x[:, n : n + step_n].astype(jnp.float32)
            else:
                e = embed(x, n)
                e = e if factor is None else e * factor
            place((rows + 1) * below, n, e)
        conv((rows - 1) * below, 1, row_scales)

    pair_copy.wait_recv()
    edge(near, 1 - odd, None, None)
    pltpu.make_async_copy(recv_far, recv_far, frecv_sem).wait()
    edge(recv_far, odd, inside, scales)

    sent = pl.ds(0, total - 1)
    pltpu.make_async_copy(recv.at[sent], recv.at[sent], send_sem).wait()
    pltpu.make_async_copy(recv_far.at[sent], recv_far.at[sent], fsend_sem).wait()
    pair_copy.wait_send()


def per_device(raw_fields, embed_weight, embed_bias, conv_weight, conv_bias):
    lat_n = lax.axis_size("lat")
    lon_n = lax.axis_size("lon")
    total = lat_n * lon_n
    var_dev, height, breadth = raw_fields.shape
    assert var_dev == 1 and lat_n % 2 == 0
    rows = height // lat_n // PATCH
    cols = breadth // lon_n // PATCH
    width = embed_weight.shape[3]
    row_slots = (cols + 2 + 15) // 16 * 16
    spare = LANES - row_slots
    assert row_slots < LANES and spare * (rows - 1) >= cols + 2
    dims = (lat_n, lon_n, height, breadth, rows, cols, width)
    group = min(lat_n, 8)
    bf16 = jnp.bfloat16
    composed = total * CELLS <= width
    tap_width = total * CELLS if composed else width
    any_space = pl.BlockSpec(memory_space=pltpu.HBM)
    vmem = pl.BlockSpec(memory_space=pltpu.VMEM)
    return pl.pallas_call(
        functools.partial(kernel, dims),
        out_shape=jax.ShapeDtypeStruct((rows, cols, width), bf16),
        in_specs=[any_space]*5,
        out_specs=vmem,
        scratch_shapes=[
            pltpu.VMEM((1, width), jnp.float32),
            pltpu.VMEM((1, width), jnp.float32),
            pltpu.VMEM((height, breadth), bf16),
            pltpu.VMEM((PATCH * group * rows * PATCH, lon_n * LANES), bf16),
            pltpu.VMEM((lat_n, lon_n, CELLS, (rows - 1) * LANES), bf16),
            pltpu.VMEM((lat_n, lon_n, CELLS, LANES), bf16),
            pltpu.VMEM((total, CELLS, (rows - 1) * LANES), bf16),
            pltpu.VMEM((total, CELLS, LANES), bf16),
            pltpu.VMEM((total, CELLS, LANES), bf16),
            pltpu.VMEM((total, PATCH, PATCH, width), bf16),
            pltpu.VMEM((total + 1, CELLS, width), bf16),
            pltpu.VMEM((3, 3, width, width), bf16),
            pltpu.VMEM((3, 3, tap_width if composed else CELLS, width), bf16),
            pltpu.VMEM((9, 8, width), jnp.float32),
            pltpu.VMEM(((rows + 2) * row_slots, 3 * tap_width), bf16),
            pltpu.SemaphoreType.DMA,
            pltpu.SemaphoreType.DMA,
            pltpu.SemaphoreType.DMA,
            pltpu.SemaphoreType.DMA,
            pltpu.SemaphoreType.DMA((9,)),
            pltpu.SemaphoreType.DMA,
            pltpu.SemaphoreType.DMA,
            pltpu.SemaphoreType.DMA,
            pltpu.SemaphoreType.DMA,
            pltpu.SemaphoreType.DMA,
            pltpu.SemaphoreType.DMA,
        ],
        compiler_params=pltpu.CompilerParams(
            collective_id=0, has_side_effects=True, vmem_limit_bytes=52 * 1024 * 1024
        ),
        name="tiles",
    )(
        *(pltpu.with_memory_space_constraint(v, pltpu.HBM) for v in (raw_fields, embed_weight, embed_bias.reshape(1, width), conv_weight, conv_bias.reshape(1, width))),
    )


def solution(mesh):
    return jax.shard_map(
        per_device,
        mesh=mesh,
        in_specs=(P(("lat", "lon"), None, None), P(), P(), P(), P()),
        out_specs=P("lat", "lon", None),
        check_vma=False,
    )
```

profile of v0, /device:TPU:0, one launch (start us, length us, event | category | flops | bytes accessed | tf_op | source)
XLA Modules:
  0.0 32.6 jit_solution(11777445558830234766)
XLA Ops:
  0.0 31.7 %tiles.1 = bf16[5,90,1024]{2,1,0:T(8,128)(2,1)S(1)} custom-call(bf16[1,160,1440]{2,1,0:T(8,128)(2,1)} %raw_hbm.1, bf16[32,4,4,1024]{3,2,1,0:T(4,128)(2,1)} %ew_hbm.1, f32[1,1024]{1,0:T(1,128)} %bitcast.2, bf16[3,3,1024,1024]{3,2,1,0:T(8,128)(2,1)} %cw_hbm.1, f32[1,1024]{1,0:T(1,128)} %bitcast.3), custom_call_target="tpu_custom_call" | custom-call | tf_op jit(solution)/shard_map/tiles/pallas_call | solution.py:319
  31.7 0.9 %copy.7 = bf16[5,90,1024]{2,1,0:T(8,128)(2,1)} copy(bf16[5,90,1024]{2,1,0:T(8,128)(2,1)S(1)} %tiles.1) | data formatting | bytes 1843200
where the time goes:
time: 32.7 us; the launch traced here: 32.6 us
  Pallas kernels  31.7 us (97%)
  local copies, waits for them, and re-layouts  0.95 us (3%)
    pallas_call x1, Pallas kernels, per_device(): pl.pallas_call(functools.partial(kernel, dims), out_shape=jax.ShapeDtypeS...  31.7 us
    unnamed x1, local copies, waits for them, and re-layouts  0.95 us

commit v1 on v0

v1 whole, which is shorter than its diff:
```python
import functools

import jax
import jax.numpy as jnp
from jax import lax
from jax.experimental import pallas as pl
from jax.experimental.pallas import tpu as pltpu
from jax.sharding import PartitionSpec as P

PATCH = 4
LANES = 128
CELLS = PATCH * PATCH
MESH = pl.DeviceIdType.MESH
STEP = 256
WINDOW = 8


def kernel(
    dims,
    raw_hbm, ew_hbm, eb_hbm, cw_hbm, cb_hbm,
    out_ref,
    eb_ref, cb_ref, raw, sides, send, send_far, recv, recv_far, near, ew_raw, ew, cw, comb, bias, taps, acc,
    eb_sem, cb_sem, raw_sem, ew_sem, cw_sem, send_sem, fsend_sem, nsend_sem,
    edge_sem, rest_sem, far_sem, near_sem,
):
    lat_n, lon_n, height, breadth, rows, cols, width = dims
    total = lat_n * lon_n
    half_n = lat_n // 2
    lat = lax.axis_index("lat")
    lon = lax.axis_index("lon")
    me = lat * lon_n + lon
    mine = lat // half_n
    odd = lat % 2
    inside = (lat > 0) & (lat < lat_n - 1)
    row_slots = taps.shape[1] // (rows + 2)
    composed = total * CELLS <= width
    tap_width = total * CELLS if composed else width
    spare = LANES - row_slots
    tail = row_slots - LANES // 2
    tiles_n = rows - 1
    last = (tiles_n - 1) * LANES
    unrolled = total <= 32

    raw_copy = pltpu.make_async_copy(raw_hbm.at[0], raw, raw_sem)
    raw_copy.start()

    def peers(other, body):
        @pl.loop(1 - other, half_n * lon_n, unroll=unrolled)
        def _(step):
            k = step // lon_n
            base = (mine + other) % 2 * half_n
            local = (k // 2 * 2 + (k + lat) % 2) if other else (lat + k) % half_n
            body(base + local, (lon + step) % lon_n)

    barrier = pltpu.get_barrier_semaphore()

    def greet(a, b):
        pl.semaphore_signal(barrier, inc=1, device_id=(a, b), device_id_type=MESH)

    peers(1, greet)
    peers(0, greet)

    ew_copy = pltpu.make_async_copy(ew_hbm, ew_raw, ew_sem)
    ew_copy.start()
    bias_copies = [
        pltpu.make_async_copy(eb_hbm, eb_ref, eb_sem),
        pltpu.make_async_copy(cb_hbm, cb_ref, cb_sem),
    ]
    for copy in bias_copies:
        copy.start()

    unit_n = width // 2
    units = 18

    def fetch(unit):
        p, q, n = unit // 6, unit // 2 % 3, pl.multiple_of(unit % 2 * unit_n, unit_n)
        return pltpu.make_async_copy(
            cw_hbm.at[p, q, :, pl.ds(n, unit_n)], cw.at[p, q, :, pl.ds(n, unit_n)], cw_sem.at[unit]
        )

    patches = breadth // PATCH
    group = min(lat_n, 8)
    group_rows = group * rows * PATCH
    block = group * CELLS
    lane = lax.broadcasted_iota(jnp.int32, (1, PATCH * LANES), 1)
    slot = lane % LANES
    cell = lane // LANES
    m = lax.broadcasted_iota(jnp.int32, (rows * block, 1), 0)
    target = (
        (m % PATCH) * group_rows
        + ((m // CELLS) % group) * (rows * PATCH)
        + (m // block) * PATCH
        + (m // PATCH) % PATCH
    )
    c = lax.broadcasted_iota(jnp.int32, (rows * block, PATCH * group_rows), 1)
    pick_rows = jnp.where(c == target, 1.0, 0.0).astype(jnp.bfloat16)
    pickers = []
    for l in range(lon_n):
        wanted = [PATCH * ((cols * l - 1 + s) % patches) for s in range(cols + 2)]
        used = sorted({x // LANES for w in wanted for x in (w, w + PATCH - 1)})
        patch = (cols * l - 1 + slot + patches) % patches
        column = jnp.where(slot < cols + 2, PATCH * patch + cell, -1)
        picks = []
        for b in used:
            k = lax.broadcasted_iota(jnp.int32, (LANES, PATCH * LANES), 0) + b * LANES
            picks.append(jnp.where(k == column, 1.0, 0.0).astype(jnp.bfloat16))
        pickers.append((used, jnp.concatenate(picks, axis=0)))

    @pl.when(jnp.logical_not(inside))
    def _():
        recv_far[...] = jnp.zeros(recv_far.shape, jnp.bfloat16)

    for unit in range(WINDOW // 2):
        fetch(unit).start()
    raw_copy.wait()
    left_half = lax.broadcasted_iota(jnp.int32, (CELLS // 2, LANES), 1) < LANES // 2
    for g in range(lat_n // group):
        for l in range(lon_n):
            used, picks = pickers[l]
            parts = []
            for b in used:
                part = raw[
                    g * group_rows : (g + 1) * group_rows,
                    b * LANES : min((b + 1) * LANES, breadth),
                ]
                short = LANES - part.shape[1]
                if short:
                    fill = jnp.zeros((group_rows, short), jnp.bfloat16)
                    part = jnp.concatenate([part, fill], axis=1)
                parts.append(part)
            found = jnp.dot(
                jnp.concatenate(parts, axis=1), picks, preferred_element_type=jnp.float32
            ).astype(jnp.bfloat16)
            for j in range(PATCH):
                sides[j * group_rows : (j + 1) * group_rows, l * LANES : (l + 1) * LANES] = (
                    found[:, j * LANES : (j + 1) * LANES]
                )
        tiles = jnp.dot(pick_rows, sides[...], preferred_element_type=jnp.float32)
        low = lax.broadcasted_iota(jnp.int32, (block, LANES), 1) < row_slots
        for l in range(lon_n):
            column = tiles[:, l * LANES : (l + 1) * LANES]
            per_row = [column[a * block : (a + 1) * block] for a in range(rows)]
            spread = per_row[rows - 2]
            here = slice(g * group, (g + 1) * group)
            for k in range(tiles_n):
                kept = per_row[k if k < rows - 2 else rows - 1]
                if k < tiles_n - 1:
                    if k * spare < row_slots:
                        kept = jnp.where(low, kept, pltpu.roll(spread, row_slots - k * spare, 1))
                    send[here, l, :, k * LANES : (k + 1) * LANES] = (
                        kept.astype(jnp.bfloat16).reshape(group, CELLS, LANES)
                    )
                else:
                    send[here, l, :, last : last + row_slots] = (
                        kept.astype(jnp.bfloat16).reshape(group, CELLS, LANES)[:, :, :row_slots]
                    )
            for t in range(group):
                at = g * group + t
                to = at + 1 if t % 2 else at - 1
                if 0 <= to < lat_n:
                    far = per_row[rows - 1 if t % 2 else 0][t * CELLS : (t + 1) * CELLS]
                    ends = pltpu.roll(far, spare, 1).astype(jnp.bfloat16)
                    send[to, l, :, last + row_slots : last + LANES] = ends[:, row_slots:]
                    folded = jnp.where(
                        left_half, far[: CELLS // 2], pltpu.roll(far[CELLS // 2 :], LANES // 2, 1)
                    )
                    send_far[to, l] = folded.astype(jnp.bfloat16)
                if at in (0, lat_n - 1):
                    send[at, l, :, last + row_slots : last + LANES] = jnp.zeros(
                        (CELLS, spare), jnp.bfloat16
                    )

    for unit in range(WINDOW // 2, WINDOW):
        fetch(unit).start()

    ew_copy.wait()
    for copy in bias_copies:
        copy.wait()
    for i in range(PATCH):
        ew[:total, PATCH * i : PATCH * (i + 1), :] = ew_raw[:, i]
    if composed:
        high = eb_ref[...].astype(jnp.bfloat16)
        rest = eb_ref[...] - high.astype(jnp.float32)
        index = lax.broadcasted_iota(jnp.int32, (CELLS, width), 0)
        both = jnp.where(index == 0, high.astype(jnp.float32), jnp.where(index == 1, rest, 0.0))
        ew[total] = both.astype(jnp.bfloat16)

    def compose(start, stop):
        @pl.loop(start, stop)
        def _(unit):
            p, q = unit // 6, unit // 2 % 3
            fetch(unit).wait()

            @pl.when(unit + WINDOW < units)
            def _():
                fetch(unit + WINDOW).start()

            if composed:
                left = ew[...].reshape((total + 1) * CELLS, width)
                for step in range(0, unit_n, STEP):
                    n = pl.multiple_of(unit % 2 * unit_n + step, STEP)
                    product = jnp.dot(
                        left, cw[p, q, :, pl.ds(n, STEP)], preferred_element_type=jnp.float32
                    )
                    comb[p, q, :, pl.ds(n, STEP)] = product[:tap_width].astype(jnp.bfloat16)
                    bias[3 * p + q, :, pl.ds(n, STEP)] = product[tap_width : tap_width + 8]

    hops = lat // 2 + odd + lon // 2
    early = (8 + hops) // (1 + hops * hops)
    compose(0, early)

    pl.semaphore_wait(barrier, total - 1)

    def edge_tile(parity):
        return pl.multiple_of((1 - parity) * last, LANES)

    def rest_tiles(parity):
        return pl.multiple_of(parity * LANES, LANES)

    def remote(source, dest, out_sem, in_sem, a, b):
        pltpu.make_async_remote_copy(
            src_ref=source, dst_ref=dest, send_sem=out_sem, recv_sem=in_sem,
            device_id=(a, b), device_id_type=MESH,
        ).start()

    def exchange(part, other):
        def body(a, b):
            if part == "edge":
                at = pl.ds(edge_tile(a % 2), LANES)
                remote(send.at[a, b, :, at], recv.at[me, :, at], send_sem, edge_sem.at[other], a, b)
            if part == "rest":
                at = pl.ds(rest_tiles(a % 2), last)
                remote(send.at[a, b, :, at], recv.at[me, :, at], send_sem, rest_sem.at[other], a, b)
            if part == "far":
                @pl.when((a > 0) & (a < lat_n - 1))
                def _():
                    remote(send_far.at[a, b], recv_far.at[me], fsend_sem, far_sem.at[other], a, b)

        peers(other, body)

    exchange("edge", 1)
    exchange("edge", 0)
    at = pl.ds(edge_tile(odd), LANES)
    pltpu.make_async_copy(send.at[lat, lon, :, at], recv.at[me, :, at], edge_sem.at[0]).start()
    at = pl.ds(rest_tiles(odd), last)
    pltpu.make_async_copy(send.at[lat, lon, :, at], recv.at[me, :, at], rest_sem.at[0]).start()

    @pl.when(inside)
    def _():
        pltpu.make_async_copy(send_far.at[lat, lon], recv_far.at[me], far_sem.at[0]).start()

    exchange("rest", 0)
    exchange("far", 0)
    exchange("rest", 1)
    exchange("far", 1)

    count = half_n * lon_n

    def sources(other):
        return pl.ds(pl.multiple_of((mine + other) % 2 * count, count), count)

    def near_copy(other):
        return pltpu.make_async_remote_copy(
            src_ref=recv.at[sources(other), :, pl.ds(edge_tile(odd), LANES)],
            dst_ref=near.at[sources(other)],
            send_sem=nsend_sem.at[other],
            recv_sem=near_sem.at[other],
            device_id=(lat + 1 - 2 * odd, lon),
            device_id_type=MESH,
        )

    def arrived(ref, sem):
        pltpu.make_async_copy(ref, ref, sem).wait()

    def forward_near(other):
        arrived(recv.at[sources(other), :, pl.ds(0, LANES)], edge_sem.at[other])
        near_copy(other).start()

    def wait_rest(other):
        arrived(recv.at[sources(other), :, pl.ds(0, last)], rest_sem.at[other])

    def wait_far(other):
        @pl.when(inside)
        def _():
            arrived(recv_far.at[sources(other)], far_sem.at[other])

    compose(early, 11)
    forward_near(0)
    compose(11, 15)
    forward_near(1)
    compose(15, units)

    groups = 2 if composed else 1
    group_width = tap_width // groups
    kernel_weights = comb if composed else cw

    def taken(ref, g):
        return ref[sources(g)] if composed else ref[...]

    def place(g, row, n, tokens):
        lanes = slice(n, n + tokens.shape[1])
        start = row * row_slots
        if not isinstance(start, int):
            start = pl.multiple_of(start, 16)
        for q in range(3):
            shifted = tokens if q == 0 else pltpu.roll(tokens, row_slots - q, 0)
            lo = q * group_width
            taps[g, pl.ds(start, row_slots), lo + lanes.start : lo + lanes.stop] = (
                shifted.astype(jnp.bfloat16)
            )

    def embed(x, n):
        if composed:
            return x[:, n : n + STEP].astype(jnp.float32)
        weights = ew[:total, :, n : n + STEP].reshape(total * CELLS, STEP)
        return jnp.dot(x, weights, preferred_element_type=jnp.float32) + eb_ref[:, n : n + STEP]

    def flat(x):
        return x.reshape(x.shape[0] * CELLS, x.shape[2]).T

    def place_rest(g):
        x = flat(taken(recv, g))
        for n in range(0, group_width, STEP):
            e = embed(x, n)
            chunks = []
            for k in range(tiles_n):
                row = k if k < rows - 2 else rows - 1
                place(g, row + 1, n, e[k * LANES : k * LANES + row_slots])
                if k * spare < row_slots:
                    chunks.append(e[k * LANES + row_slots : (k + 1) * LANES])
            place(g, rows - 1, n, jnp.concatenate(chunks, axis=0)[:row_slots])

    def place_near(g):
        x = flat(taken(near, g))[:row_slots]
        for n in range(0, group_width, STEP):
            place(g, (rows + 1) * (1 - odd), n, embed(x, n))

    def place_far(g):
        folded = taken(recv_far, g).astype(jnp.float32)
        n_src = folded.shape[0]
        turned = pltpu.roll(folded.reshape(n_src * CELLS // 2, LANES), LANES // 2, 1)
        whole = jnp.concatenate([folded, turned.reshape(folded.shape)], axis=1)
        x = flat(whole)[: LANES // 2].astype(jnp.bfloat16)
        edge = recv[sources(g), :, last:] if composed else recv[:, :, last:]
        ends = flat(edge)[row_slots : row_slots + tail]
        x = jnp.concatenate([x, ends], axis=0)
        for n in range(0, group_width, STEP):
            e = embed(x, n)
            if not composed:
                e = e * jnp.where(inside, 1.0, 0.0)
            place(g, (rows + 1) * odd, n, e)

    top = jnp.where(lat > 0, 1.0, 0.0)
    bottom = jnp.where(lat < lat_n - 1, 1.0, 0.0)

    def row_bias(n, scales):
        total_bias = cb_ref[:, pl.ds(n, STEP)]
        if composed:
            for p in range(3):
                part = 0.0
                for q in range(3):
                    part += bias[3 * p + q, 0:1, pl.ds(n, STEP)] + bias[3 * p + q, 1:2, pl.ds(n, STEP)]
                total_bias = total_bias + part * scales[p]
        return total_bias

    def rows_at(a, n_rows):
        return pl.ds(pl.multiple_of(a * row_slots, 16), n_rows * row_slots)

    def conv(g, a, n_rows, first, final):
        @pl.loop(0, width // (2 * STEP))
        def _(block_n):
            for part_n in range(2):
                n = pl.multiple_of(block_n * (2 * STEP) + part_n * STEP, STEP)
                at_n = pl.ds(n, STEP)
                summed = None
                for p in range(3):
                    if composed:
                        chosen = pl.ds(pl.multiple_of((mine + g) % 2 * group_width, group_width), group_width)
                        weights = kernel_weights[p, :, chosen, at_n]
                    else:
                        weights = kernel_weights[p, :, :, at_n]
                    part = jnp.dot(
                        taps[g, rows_at(a + p, n_rows), :],
                        weights.reshape(3 * group_width, STEP),
                        preferred_element_type=jnp.float32,
                    )
                    summed = part if summed is None else summed + part
                if first:
                    shift = row_bias(n, (1.0, 1.0, 1.0))
                    above, below = row_bias(n, (top, 1.0, 1.0)), row_bias(n, (1.0, 1.0, bottom))
                for k in range(n_rows):
                    value = summed[k * row_slots : (k + 1) * row_slots]
                    if first:
                        value = value + (above if k == 0 else below if k == rows - 1 else shift)
                    else:
                        value = value + acc[rows_at(a + k, 1), at_n]
                    if final:
                        value = 0.5 * value * (1.0 + lax.erf(value * (0.5 ** 0.5)))
                        out_ref[a + k, :, at_n] = value[:cols].astype(jnp.bfloat16)
                    else:
                        acc[rows_at(a + k, 1), at_n] = value

    main_row, far_row = 1 - odd, (rows - 1) * odd
    if composed:
        wait_rest(0)
        place_rest(0)
        near_copy(0).wait_recv()
        place_near(0)
        wait_far(0)
        place_far(0)
        conv(0, 0, rows, True, False)
        wait_rest(1)
        place_rest(1)
        near_copy(1).wait_recv()
        place_near(1)
        conv(1, main_row, rows - 1, False, True)
        wait_far(1)
        place_far(1)
        conv(1, far_row, 1, False, True)
    else:
        for other in range(2):
            wait_rest(other)
            near_copy(other).wait_recv()
            wait_far(other)
        place_rest(0)
        place_near(0)
        place_far(0)
        conv(0, 0, rows, True, True)

    sent = pl.ds(0, total - 1)
    arrived(recv.at[sent], send_sem)
    targets = (lat_n - 2) * lon_n

    @pl.when(inside)
    def _():
        arrived(recv_far.at[pl.ds(0, targets - 1)], fsend_sem)

    @pl.when(jnp.logical_not(inside))
    def _():
        arrived(recv_far.at[pl.ds(0, targets)], fsend_sem)

    near_copy(0).wait_send()
    near_copy(1).wait_send()


def per_device(raw_fields, embed_weight, embed_bias, conv_weight, conv_bias):
    lat_n = lax.axis_size("lat")
    lon_n = lax.axis_size("lon")
    total = lat_n * lon_n
    var_dev, height, breadth = raw_fields.shape
    assert var_dev == 1 and lat_n % 4 == 0
    rows = height // lat_n // PATCH
    cols = breadth // lon_n // PATCH
    width = embed_weight.shape[3]
    row_slots = (cols + 2 + 15) // 16 * 16
    spare = LANES - row_slots
    assert LANES // 2 < row_slots < LANES and spare * (rows - 2) >= row_slots
    assert row_slots - LANES // 2 <= spare
    dims = (lat_n, lon_n, height, breadth, rows, cols, width)
    group = min(lat_n, 8)
    bf16 = jnp.bfloat16
    composed = total * CELLS <= width
    tap_width = total * CELLS if composed else width
    groups = 2 if composed else 1
    any_space = pl.BlockSpec(memory_space=pltpu.HBM)
    vmem = pl.BlockSpec(memory_space=pltpu.VMEM)
    return pl.pallas_call(
        functools.partial(kernel, dims),
        out_shape=jax.ShapeDtypeStruct((rows, cols, width), bf16),
        in_specs=[any_space]*5,
        out_specs=vmem,
        scratch_shapes=[
            pltpu.VMEM((1, width), jnp.float32),
            pltpu.VMEM((1, width), jnp.float32),
            pltpu.VMEM((height, breadth), bf16),
            pltpu.VMEM((PATCH * group * rows * PATCH, lon_n * LANES), bf16),
            pltpu.VMEM((lat_n, lon_n, CELLS, (rows - 1) * LANES), bf16),
            pltpu.VMEM((lat_n, lon_n, CELLS // 2, LANES), bf16),
            pltpu.VMEM((total, CELLS, (rows - 1) * LANES), bf16),
            pltpu.VMEM((total, CELLS // 2, LANES), bf16),
            pltpu.VMEM((total, CELLS, LANES), bf16),
            pltpu.VMEM((total, PATCH, PATCH, width), bf16),
            pltpu.VMEM((total + 1, CELLS, width), bf16),
            pltpu.VMEM((3, 3, width, width), bf16),
            pltpu.VMEM((3, 3, tap_width if composed else CELLS, width), bf16),
            pltpu.VMEM((9, 8, width), jnp.float32),
            pltpu.VMEM((groups, (rows + 2) * row_slots, 3 * tap_width // groups), bf16),
            pltpu.VMEM((rows * row_slots, width if composed else LANES), jnp.float32),
            pltpu.SemaphoreType.DMA,
            pltpu.SemaphoreType.DMA,
            pltpu.SemaphoreType.DMA,
            pltpu.SemaphoreType.DMA,
            pltpu.SemaphoreType.DMA((18,)),
            pltpu.SemaphoreType.DMA,
            pltpu.SemaphoreType.DMA,
            pltpu.SemaphoreType.DMA((2,)),
            pltpu.SemaphoreType.DMA((2,)),
            pltpu.SemaphoreType.DMA((2,)),
            pltpu.SemaphoreType.DMA((2,)),
            pltpu.SemaphoreType.DMA((2,)),
        ],
        compiler_params=pltpu.CompilerParams(
            collective_id=0, has_side_effects=True, vmem_limit_bytes=50 * 1024 * 1024
        ),
        name="tiles",
    )(
        *(pltpu.with_memory_space_constraint(v, pltpu.HBM) for v in (raw_fields, embed_weight, embed_bias.reshape(1, width), conv_weight, conv_bias.reshape(1, width))),
    )


def solution(mesh):
    return jax.shard_map(
        per_device,
        mesh=mesh,
        in_specs=(P(("lat", "lon"), None, None), P(), P(), P(), P()),
        out_specs=P("lat", "lon", None),
        check_vma=False,
    )
```

time: 32.7 us -> 26 us (0.80)
  Pallas kernels: 31.7 us -> 24.8 us
    pallas_call x1, Pallas kernels: 31.7 us -> 24.8 us  [per_device(): pl.pallas_call(functools.partial(kernel, dims), out_shape=jax.ShapeDtypeS...]
where the time goes in v1:
time: 26 us; the launch traced here: 25.8 us
  Pallas kernels  24.8 us (95%)
  local copies, waits for them, and re-layouts  0.95 us (4%)
    pallas_call x1, Pallas kernels, per_device(): pl.pallas_call(functools.partial(kernel, dims), out_shape=jax.ShapeDtypeS...  24.8 us
    unnamed x1, local copies, waits for them, and re-layouts  0.95 us

profile of v1, /device:TPU:0, one launch (start us, length us, event | category | flops | bytes accessed | tf_op | source)
XLA Modules:
  0.0 25.8 jit_solution(13338413494979642817)
XLA Ops:
  0.0 24.8 %tiles.1 = bf16[5,90,1024]{2,1,0:T(8,128)(2,1)S(1)} custom-call(bf16[1,160,1440]{2,1,0:T(8,128)(2,1)} %raw_hbm.1, bf16[32,4,4,1024]{3,2,1,0:T(4,128)(2,1)} %ew_hbm.1, f32[1,1024]{1,0:T(1,128)} %bitcast.2, bf16[3,3,1024,1024]{3,2,1,0:T(8,128)(2,1)} %cw_hbm.1, f32[1,1024]{1,0:T(1,128)} %bitcast.3), custom_call_target="tpu_custom_call" | custom-call | tf_op jit(solution)/shard_map/tiles/pallas_call | solution.py:467
  24.9 0.9 %copy.7 = bf16[5,90,1024]{2,1,0:T(8,128)(2,1)} copy(bf16[5,90,1024]{2,1,0:T(8,128)(2,1)S(1)} %tiles.1) | data formatting | bytes 1843200

commit v2 on v1

--- a/solution.py
+++ b/solution.py
@@ -12,14 +12,15 @@
 CELLS = PATCH * PATCH
 MESH = pl.DeviceIdType.MESH
 STEP = 256
-WINDOW = 8
+WINDOW = 9
+FIRST = 6
 
 
 def kernel(
     dims,
     raw_hbm, ew_hbm, eb_hbm, cw_hbm, cb_hbm,
     out_ref,
-    eb_ref, cb_ref, raw, sides, send, send_far, recv, recv_far, near, ew_raw, ew, cw, comb, bias, taps, acc,
+    eb_ref, cb_ref, raw, sides, send, send_far, far_ends, recv, recv_far, near, ew_raw, ew, cw, comb, bias, taps, acc,
     eb_sem, cb_sem, raw_sem, ew_sem, cw_sem, send_sem, fsend_sem, nsend_sem,
     edge_sem, rest_sem, far_sem, near_sem,
 ):
@@ -110,7 +111,7 @@
     def _():
         recv_far[...] = jnp.zeros(recv_far.shape, jnp.bfloat16)
 
-    for unit in range(WINDOW // 2):
+    for unit in range(FIRST):
         fetch(unit).start()
     raw_copy.wait()
     left_half = lax.broadcasted_iota(jnp.int32, (CELLS // 2, LANES), 1) < LANES // 2
@@ -137,40 +138,39 @@
                 )
         tiles = jnp.dot(pick_rows, sides[...], preferred_element_type=jnp.float32)
         low = lax.broadcasted_iota(jnp.int32, (block, LANES), 1) < row_slots
+        even = lax.broadcasted_iota(jnp.int32, (block, LANES), 0) // CELLS % 2 == 0
         for l in range(lon_n):
             column = tiles[:, l * LANES : (l + 1) * LANES]
             per_row = [column[a * block : (a + 1) * block] for a in range(rows)]
             spread = per_row[rows - 2]
             here = slice(g * group, (g + 1) * group)
+            turned = [pltpu.roll(spread, row_slots - k * spare, 1) for k in range(tiles_n - 1)]
             for k in range(tiles_n):
                 kept = per_row[k if k < rows - 2 else rows - 1]
-                if k < tiles_n - 1:
-                    if k * spare < row_slots:
-                        kept = jnp.where(low, kept, pltpu.roll(spread, row_slots - k * spare, 1))
-                    send[here, l, :, k * LANES : (k + 1) * LANES] = (
-                        kept.astype(jnp.bfloat16).reshape(group, CELLS, LANES)
-                    )
-                else:
-                    send[here, l, :, last : last + row_slots] = (
-                        kept.astype(jnp.bfloat16).reshape(group, CELLS, LANES)[:, :, :row_slots]
-                    )
+                kept = jnp.where(
+                    low, kept, jnp.where(even, turned[min(k, tiles_n - 2)], turned[max(k - 1, 0)])
+                )
+                send[here, l, :, k * LANES : (k + 1) * LANES] = (
+                    kept.astype(jnp.bfloat16).reshape(group, CELLS, LANES)
+                )
             for t in range(group):
                 at = g * group + t
                 to = at + 1 if t % 2 else at - 1
                 if 0 <= to < lat_n:
                     far = per_row[rows - 1 if t % 2 else 0][t * CELLS : (t + 1) * CELLS]
                     ends = pltpu.roll(far, spare, 1).astype(jnp.bfloat16)
-                    send[to, l, :, last + row_slots : last + LANES] = ends[:, row_slots:]
+                    far_ends[to, l, :, row_slots:] = ends[:, row_slots:]
                     folded = jnp.where(
                         left_half, far[: CELLS // 2], pltpu.roll(far[CELLS // 2 :], LANES // 2, 1)
                     )
                     send_far[to, l] = folded.astype(jnp.bfloat16)
                 if at in (0, lat_n - 1):
-                    send[at, l, :, last + row_slots : last + LANES] = jnp.zeros(
-                        (CELLS, spare), jnp.bfloat16
-                    )
-
-    for unit in range(WINDOW // 2, WINDOW):
+                    far_ends[at, l, :, row_slots:] = jnp.zeros((CELLS, spare), jnp.bfloat16)
+    for t in range(lat_n):
+        tile = 0 if t % 2 else last
+        send[t, :, :, tile + row_slots : tile + LANES] = far_ends[t, :, :, row_slots:]
+
+    for unit in range(FIRST, WINDOW):
         fetch(unit).start()
 
     ew_copy.wait()
@@ -186,30 +186,21 @@
         ew[total] = both.astype(jnp.bfloat16)
 
     def compose(start, stop):
-        @pl.loop(start, stop)
-        def _(unit):
-            p, q = unit // 6, unit // 2 % 3
+        for unit in range(start, stop):
             fetch(unit).wait()
-
-            @pl.when(unit + WINDOW < units)
-            def _():
-                fetch(unit + WINDOW).start()
-
-            if composed:
-                left = ew[...].reshape((total + 1) * CELLS, width)
+        for unit in range(start + WINDOW, min(stop + WINDOW, units)):
+            fetch(unit).start()
+        if composed:
+            left = ew[...].reshape((total + 1) * CELLS, width)
+            for unit in range(start, stop):
+                p, q = unit // 6, unit // 2 % 3
                 for step in range(0, unit_n, STEP):
-                    n = pl.multiple_of(unit % 2 * unit_n + step, STEP)
+                    n = unit % 2 * unit_n + step
                     product = jnp.dot(
-                        left, cw[p, q, :, pl.ds(n, STEP)], preferred_element_type=jnp.float32
+                        left, cw[p, q, :, n : n + STEP], preferred_element_type=jnp.float32
                     )
-                    comb[p, q, :, pl.ds(n, STEP)] = product[:tap_width].astype(jnp.bfloat16)
-                    bias[3 * p + q, :, pl.ds(n, STEP)] = product[tap_width : tap_width + 8]
-
-    hops = lat // 2 + odd + lon // 2
-    early = (8 + hops) // (1 + hops * hops)
-    compose(0, early)
-
-    pl.semaphore_wait(barrier, total - 1)
+                    comb[p, q, :, n : n + STEP] = product[:tap_width].astype(jnp.bfloat16)
+                    bias[3 * p + q, :, n : n + STEP] = product[tap_width : tap_width + 8]
 
     def edge_tile(parity):
         return pl.multiple_of((1 - parity) * last, LANES)
@@ -228,6 +219,10 @@
             if part == "edge":
                 at = pl.ds(edge_tile(a % 2), LANES)
                 remote(send.at[a, b, :, at], recv.at[me, :, at], send_sem, edge_sem.at[other], a, b)
+            if part == "near":
+                at = pl.ds(edge_tile(1 - a % 2), LANES)
+                source = send.at[a + 1 - 2 * (a % 2), b, :, at]
+                remote(source, near.at[me], nsend_sem.at[0], near_sem.at[0], a, b)
             if part == "rest":
                 at = pl.ds(rest_tiles(a % 2), last)
                 remote(send.at[a, b, :, at], recv.at[me, :, at], send_sem, rest_sem.at[other], a, b)
@@ -238,33 +233,39 @@
 
         peers(other, body)
 
-    exchange("edge", 1)
-    exchange("edge", 0)
-    at = pl.ds(edge_tile(odd), LANES)
-    pltpu.make_async_copy(send.at[lat, lon, :, at], recv.at[me, :, at], edge_sem.at[0]).start()
-    at = pl.ds(rest_tiles(odd), last)
-    pltpu.make_async_copy(send.at[lat, lon, :, at], recv.at[me, :, at], rest_sem.at[0]).start()
-
-    @pl.when(inside)
-    def _():
-        pltpu.make_async_copy(send_far.at[lat, lon], recv_far.at[me], far_sem.at[0]).start()
-
-    exchange("rest", 0)
-    exchange("far", 0)
-    exchange("rest", 1)
-    exchange("far", 1)
+    def issue():
+        pl.semaphore_wait(barrier, total - 1)
+        exchange("edge", 1)
+        exchange("edge", 0)
+        exchange("near", 0)
+        exchange("far", 0)
+        exchange("far", 1)
+        exchange("rest", 0)
+        exchange("rest", 1)
+        own = pl.ds(edge_tile(odd), LANES)
+        pltpu.make_async_copy(send.at[lat, lon, :, own], recv.at[me, :, own], edge_sem.at[0]).start()
+        pair = pl.ds(edge_tile(1 - odd), LANES)
+        pltpu.make_async_copy(
+            send.at[lat + 1 - 2 * odd, lon, :, pair], near.at[me], near_sem.at[0]
+        ).start()
+        own = pl.ds(rest_tiles(odd), last)
+        pltpu.make_async_copy(send.at[lat, lon, :, own], recv.at[me, :, own], rest_sem.at[0]).start()
+
+        @pl.when(inside)
+        def _():
+            pltpu.make_async_copy(send_far.at[lat, lon], recv_far.at[me], far_sem.at[0]).start()
 
     count = half_n * lon_n
 
     def sources(other):
         return pl.ds(pl.multiple_of((mine + other) % 2 * count, count), count)
 
-    def near_copy(other):
+    def near_copy():
         return pltpu.make_async_remote_copy(
-            src_ref=recv.at[sources(other), :, pl.ds(edge_tile(odd), LANES)],
-            dst_ref=near.at[sources(other)],
-            send_sem=nsend_sem.at[other],
-            recv_sem=near_sem.at[other],
+            src_ref=recv.at[sources(1), :, pl.ds(edge_tile(odd), LANES)],
+            dst_ref=near.at[sources(1)],
+            send_sem=nsend_sem.at[1],
+            recv_sem=near_sem.at[1],
             device_id=(lat + 1 - 2 * odd, lon),
             device_id_type=MESH,
         )
@@ -272,9 +273,15 @@
     def arrived(ref, sem):
         pltpu.make_async_copy(ref, ref, sem).wait()
 
-    def forward_near(other):
+    def wait_edge(other):
         arrived(recv.at[sources(other), :, pl.ds(0, LANES)], edge_sem.at[other])
-        near_copy(other).start()
+
+    def forward_near():
+        wait_edge(1)
+        near_copy().start()
+
+    def wait_near(other):
+        arrived(near.at[sources(other)], near_sem.at[other])
 
     def wait_rest(other):
         arrived(recv.at[sources(other), :, pl.ds(0, last)], rest_sem.at[other])
@@ -284,10 +291,14 @@
         def _():
             arrived(recv_far.at[sources(other)], far_sem.at[other])
 
-    compose(early, 11)
-    forward_near(0)
-    compose(11, 15)
-    forward_near(1)
+    hops = lat // 2 + odd + lon // 2
+    early = (0, 2, 4, 8)
+    for k, stop in enumerate(early):
+        if k:
+            compose(early[k - 1], stop)
+        pl.when(jnp.maximum(len(early) - 1 - hops, 0) == k)(issue)
+    compose(early[-1], 15)
+    forward_near()
     compose(15, units)
 
     groups = 2 if composed else 1
@@ -326,9 +337,11 @@
             for k in range(tiles_n):
                 row = k if k < rows - 2 else rows - 1
                 place(g, row + 1, n, e[k * LANES : k * LANES + row_slots])
-                if k * spare < row_slots:
-                    chunks.append(e[k * LANES + row_slots : (k + 1) * LANES])
-            place(g, rows - 1, n, jnp.concatenate(chunks, axis=0)[:row_slots])
+                chunks.append(e[k * LANES + row_slots : (k + 1) * LANES])
+            kept = [
+                jnp.where(odd > 0, chunks[k + 1], chunks[k]) for k in range(tiles_n - 1)
+            ]
+            place(g, rows - 1, n, jnp.concatenate(kept, axis=0)[:row_slots])
 
     def place_near(g):
         x = flat(taken(near, g))[:row_slots]
@@ -341,7 +354,8 @@
         turned = pltpu.roll(folded.reshape(n_src * CELLS // 2, LANES), LANES // 2, 1)
         whole = jnp.concatenate([folded, turned.reshape(folded.shape)], axis=1)
         x = flat(whole)[: LANES // 2].astype(jnp.bfloat16)
-        edge = recv[sources(g), :, last:] if composed else recv[:, :, last:]
+        at = pl.ds(edge_tile(odd), LANES)
+        edge = recv[sources(g), :, at] if composed else recv[:, :, at]
         ends = flat(edge)[row_slots : row_slots + tail]
         x = jnp.concatenate([x, ends], axis=0)
         for n in range(0, group_width, STEP):
@@ -367,10 +381,10 @@
         return pl.ds(pl.multiple_of(a * row_slots, 16), n_rows * row_slots)
 
     def conv(g, a, n_rows, first, final):
-        @pl.loop(0, width // (2 * STEP))
+        @pl.loop(0, 1)
         def _(block_n):
-            for part_n in range(2):
-                n = pl.multiple_of(block_n * (2 * STEP) + part_n * STEP, STEP)
+            for part_n in range(width // STEP):
+                n = part_n * STEP
                 at_n = pl.ds(n, STEP)
                 summed = None
                 for p in range(3):
@@ -400,27 +414,27 @@
                     else:
                         acc[rows_at(a + k, 1), at_n] = value
 
-    main_row, far_row = 1 - odd, (rows - 1) * odd
     if composed:
+        wait_edge(0)
+        wait_near(0)
+        wait_far(0)
+        place_near(0)
+        place_far(0)
         wait_rest(0)
         place_rest(0)
-        near_copy(0).wait_recv()
-        place_near(0)
-        wait_far(0)
-        place_far(0)
         conv(0, 0, rows, True, False)
+        wait_near(1)
+        wait_far(1)
+        place_near(1)
+        place_far(1)
         wait_rest(1)
         place_rest(1)
-        near_copy(1).wait_recv()
-        place_near(1)
-        conv(1, main_row, rows - 1, False, True)
-        wait_far(1)
-        place_far(1)
-        conv(1, far_row, 1, False, True)
+        conv(1, 0, rows, False, True)
     else:
+        wait_edge(0)
         for other in range(2):
             wait_rest(other)
-            near_copy(other).wait_recv()
+            wait_near(other)
             wait_far(other)
         place_rest(0)
         place_near(0)
@@ -439,8 +453,8 @@
     def _():
         arrived(recv_far.at[pl.ds(0, targets)], fsend_sem)
 
-    near_copy(0).wait_send()
-    near_copy(1).wait_send()
+    arrived(near.at[pl.ds(0, count - 1)], nsend_sem.at[0])
+    near_copy().wait_send()
 
 
 def per_device(raw_fields, embed_weight, embed_bias, conv_weight, conv_bias):
@@ -454,7 +468,7 @@
     width = embed_weight.shape[3]
     row_slots = (cols + 2 + 15) // 16 * 16
     spare = LANES - row_slots
-    assert LANES // 2 < row_slots < LANES and spare * (rows - 2) >= row_slots
+    assert LANES // 2 < row_slots < LANES and spare * (rows - 2) == row_slots
     assert row_slots - LANES // 2 <= spare
     dims = (lat_n, lon_n, height, breadth, rows, cols, width)
     group = min(lat_n, 8)
@@ -476,6 +490,7 @@
             pltpu.VMEM((PATCH * group * rows * PATCH, lon_n * LANES), bf16),
             pltpu.VMEM((lat_n, lon_n, CELLS, (rows - 1) * LANES), bf16),
             pltpu.VMEM((lat_n, lon_n, CELLS // 2, LANES), bf16),
+            pltpu.VMEM((lat_n, lon_n, CELLS, LANES), bf16),
             pltpu.VMEM((total, CELLS, (rows - 1) * LANES), bf16),
             pltpu.VMEM((total, CELLS // 2, LANES), bf16),
             pltpu.VMEM((total, CELLS, LANES), bf16),

time: 26 us -> 23.9 us (0.919)
  the two profiles are of different devices: /device:TPU:0 before, /device:TPU:5 now
where the time goes in v2:
time: 23.9 us; the launch traced here: 23.7 us
  Pallas kernels  22.8 us (95%)
  local copies, waits for them, and re-layouts  0.95 us (4%)
    pallas_call x1, Pallas kernels, per_device(): pl.pallas_call(functools.partial(kernel, dims), out_shape=jax.ShapeDtypeS...  22.8 us
    unnamed x1, local copies, waits for them, and re-layouts  0.95 us

profile of v2, /device:TPU:5, one launch (start us, length us, event | category | flops | bytes accessed | tf_op | source)
XLA Modules:
  0.0 23.7 jit_solution(1509367204012384138)
XLA Ops:
  0.0 22.8 %tiles.1 = bf16[5,90,1024]{2,1,0:T(8,128)(2,1)S(1)} custom-call(bf16[1,160,1440]{2,1,0:T(8,128)(2,1)} %raw_hbm.1, bf16[32,4,4,1024]{3,2,1,0:T(4,128)(2,1)} %ew_hbm.1, f32[1,1024]{1,0:T(1,128)} %bitcast.2, bf16[3,3,1024,1024]{3,2,1,0:T(8,128)(2,1)} %cw_hbm.1, f32[1,1024]{1,0:T(1,128)} %bitcast.3), custom_call_target="tpu_custom_call" | custom-call | tf_op jit(solution)/shard_map/tiles/pallas_call | solution.py:481
  22.8 0.9 %copy.7 = bf16[5,90,1024]{2,1,0:T(8,128)(2,1)} copy(bf16[5,90,1024]{2,1,0:T(8,128)(2,1)S(1)} %tiles.1) | data formatting | bytes 1843200

commit v3 on v2

--- a/solution.py
+++ b/solution.py
@@ -14,13 +14,14 @@
 STEP = 256
 WINDOW = 9
 FIRST = 6
+FORWARD = (11, 14)
 
 
 def kernel(
     dims,
     raw_hbm, ew_hbm, eb_hbm, cw_hbm, cb_hbm,
     out_ref,
-    eb_ref, cb_ref, raw, sides, send, send_far, far_ends, recv, recv_far, near, ew_raw, ew, cw, comb, bias, taps, acc,
+    eb_ref, cb_ref, raw, sides, send, send_far, far_ends, recv, recv_far, near, ew_raw, ew, cw, comb, bias, taps, nine, acc,
     eb_sem, cb_sem, raw_sem, ew_sem, cw_sem, send_sem, fsend_sem, nsend_sem,
     edge_sem, rest_sem, far_sem, near_sem,
 ):
@@ -33,7 +34,7 @@
     mine = lat // half_n
     odd = lat % 2
     inside = (lat > 0) & (lat < lat_n - 1)
-    row_slots = taps.shape[1] // (rows + 2)
+    row_slots = taps.shape[0] // (rows + 2)
     composed = total * CELLS <= width
     tap_width = total * CELLS if composed else width
     spare = LANES - row_slots
@@ -50,7 +51,7 @@
         def _(step):
             k = step // lon_n
             base = (mine + other) % 2 * half_n
-            local = (k // 2 * 2 + (k + lat) % 2) if other else (lat + k) % half_n
+            local = k if other else (lat + k) % half_n
             body(base + local, (lon + step) % lon_n)
 
     barrier = pltpu.get_barrier_semaphore()
@@ -214,6 +215,13 @@
             device_id=(a, b), device_id_type=MESH,
         ).start()
 
+    quarter_n = lat_n // 4
+    quarter = lat // quarter_n
+
+    def relation(a):
+        there = a // quarter_n
+        return (there // 2 + quarter // 2) % 2 * 2 + (there + quarter) % 2
+
     def exchange(part, other):
         def body(a, b):
             if part == "edge":
@@ -225,7 +233,7 @@
                 remote(source, near.at[me], nsend_sem.at[0], near_sem.at[0], a, b)
             if part == "rest":
                 at = pl.ds(rest_tiles(a % 2), last)
-                remote(send.at[a, b, :, at], recv.at[me, :, at], send_sem, rest_sem.at[other], a, b)
+                remote(send.at[a, b, :, at], recv.at[me, :, at], send_sem, rest_sem.at[relation(a)], a, b)
             if part == "far":
                 @pl.when((a > 0) & (a < lat_n - 1))
                 def _():
@@ -283,8 +291,8 @@
     def wait_near(other):
         arrived(near.at[sources(other)], near_sem.at[other])
 
-    def wait_rest(other):
-        arrived(recv.at[sources(other), :, pl.ds(0, last)], rest_sem.at[other])
+    def wait_rest(rel):
+        arrived(recv.at[pl.ds(0, count // 2), :, pl.ds(0, last)], rest_sem.at[rel])
 
     def wait_far(other):
         @pl.when(inside)
@@ -292,46 +300,73 @@
             arrived(recv_far.at[sources(other)], far_sem.at[other])
 
     hops = lat // 2 + odd + lon // 2
-    early = (0, 2, 4, 8)
+    early = (0, 1, 3, 6)
     for k, stop in enumerate(early):
         if k:
             compose(early[k - 1], stop)
         pl.when(jnp.maximum(len(early) - 1 - hops, 0) == k)(issue)
-    compose(early[-1], 15)
-    forward_near()
-    compose(15, units)
-
-    groups = 2 if composed else 1
-    group_width = tap_width // groups
-    kernel_weights = comb if composed else cw
-
-    def taken(ref, g):
-        return ref[sources(g)] if composed else ref[...]
+    compose(early[-1], FORWARD[0])
+    pl.when(hops > 0)(forward_near)
+    compose(FORWARD[0], FORWARD[1])
+    pl.when(hops == 0)(forward_near)
+    compose(FORWARD[1], units)
+
+    group_width = tap_width // 2 if composed else tap_width
+    quarter_width = tap_width // 4
+    middle = jnp.where(quarter < lat_n // quarter_n - 1, 2, 3)
+    stages = ((0,), (1, middle), (5 - middle,))
+
+    def quarter_of(rel):
+        return (quarter // 2 + rel // 2) % 2 * 2 + (quarter + rel) % 2
+
+    def part_of(rel, size):
+        return pl.ds(pl.multiple_of(quarter_of(rel) * size, size), size)
+
+    def taken(ref, g, at=slice(None)):
+        if not composed:
+            return ref[:, :, at]
+        return jnp.concatenate(
+            [ref[part_of(rel, count // 2), :, at] for rel in stages[g]], axis=0
+        )
 
     def place(g, row, n, tokens):
-        lanes = slice(n, n + tokens.shape[1])
-        start = row * row_slots
-        if not isinstance(start, int):
-            start = pl.multiple_of(start, 16)
         for q in range(3):
             shifted = tokens if q == 0 else pltpu.roll(tokens, row_slots - q, 0)
-            lo = q * group_width
-            taps[g, pl.ds(start, row_slots), lo + lanes.start : lo + lanes.stop] = (
-                shifted.astype(jnp.bfloat16)
-            )
+            shifted = shifted.astype(jnp.bfloat16)
+            if g == 1 or not composed:
+                start = row * row_slots
+                if not isinstance(start, int):
+                    start = pl.multiple_of(start, 16)
+                lo = q * group_width + n
+                taps[pl.ds(start, row_slots), lo : lo + tokens.shape[1]] = shifted
+                continue
+            if isinstance(row, int):
+                targets = [(row - p, p) for p in range(3) if 0 <= row - p < rows]
+            else:
+                below = row // (rows + 1)
+                targets = [((rows - 1) * below, 2 * below)]
+            for at_row, p in targets:
+                start = at_row * row_slots
+                lo = (3 * p + q) * quarter_width
+                if not isinstance(row, int):
+                    start, lo = pl.multiple_of(start, 16), pl.multiple_of(lo, LANES)
+                nine[g // 2, pl.ds(start, row_slots), pl.ds(lo, quarter_width)] = shifted
 
     def embed(x, n):
         if composed:
-            return x[:, n : n + STEP].astype(jnp.float32)
+            return x.astype(jnp.float32)
         weights = ew[:total, :, n : n + STEP].reshape(total * CELLS, STEP)
         return jnp.dot(x, weights, preferred_element_type=jnp.float32) + eb_ref[:, n : n + STEP]
 
+    def spans(g):
+        return (0,) if composed else range(0, group_width, STEP)
+
     def flat(x):
         return x.reshape(x.shape[0] * CELLS, x.shape[2]).T
 
     def place_rest(g):
         x = flat(taken(recv, g))
-        for n in range(0, group_width, STEP):
+        for n in spans(g):
             e = embed(x, n)
             chunks = []
             for k in range(tiles_n):
@@ -345,7 +380,7 @@
 
     def place_near(g):
         x = flat(taken(near, g))[:row_slots]
-        for n in range(0, group_width, STEP):
+        for n in spans(g):
             place(g, (rows + 1) * (1 - odd), n, embed(x, n))
 
     def place_far(g):
@@ -355,10 +390,10 @@
         whole = jnp.concatenate([folded, turned.reshape(folded.shape)], axis=1)
         x = flat(whole)[: LANES // 2].astype(jnp.bfloat16)
         at = pl.ds(edge_tile(odd), LANES)
-        edge = recv[sources(g), :, at] if composed else recv[:, :, at]
+        edge = taken(recv, g, at)
         ends = flat(edge)[row_slots : row_slots + tail]
         x = jnp.concatenate([x, ends], axis=0)
-        for n in range(0, group_width, STEP):
+        for n in spans(g):
             e = embed(x, n)
             if not composed:
                 e = e * jnp.where(inside, 1.0, 0.0)
@@ -386,19 +421,28 @@
             for part_n in range(width // STEP):
                 n = part_n * STEP
                 at_n = pl.ds(n, STEP)
-                summed = None
-                for p in range(3):
-                    if composed:
-                        chosen = pl.ds(pl.multiple_of((mine + g) % 2 * group_width, group_width), group_width)
-                        weights = kernel_weights[p, :, chosen, at_n]
-                    else:
-                        weights = kernel_weights[p, :, :, at_n]
-                    part = jnp.dot(
-                        taps[g, rows_at(a + p, n_rows), :],
-                        weights.reshape(3 * group_width, STEP),
+                if composed and g != 1:
+                    weights = comb[:, :, part_of(stages[g][0], quarter_width), at_n]
+                    summed = jnp.dot(
+                        nine[g // 2], weights.reshape(9 * quarter_width, STEP),
                         preferred_element_type=jnp.float32,
                     )
-                    summed = part if summed is None else summed + part
+                else:
+                    summed = None
+                    for p in range(3):
+                        if composed:
+                            weights = jnp.concatenate(
+                                [comb[p, :, part_of(rel, quarter_width), at_n] for rel in stages[g]],
+                                axis=1,
+                            )
+                        else:
+                            weights = cw[p, :, :, at_n]
+                        part = jnp.dot(
+                            taps[rows_at(a + p, n_rows), :],
+                            weights.reshape(3 * group_width, STEP),
+                            preferred_element_type=jnp.float32,
+                        )
+                        summed = part if summed is None else summed + part
                 if first:
                     shift = row_bias(n, (1.0, 1.0, 1.0))
                     above, below = row_bias(n, (top, 1.0, 1.0)), row_bias(n, (1.0, 1.0, bottom))
@@ -414,26 +458,32 @@
                     else:
                         acc[rows_at(a + k, 1), at_n] = value
 
+    wait_edge(0)
     if composed:
-        wait_edge(0)
         wait_near(0)
         wait_far(0)
+        wait_rest(0)
+        place_rest(0)
         place_near(0)
         place_far(0)
-        wait_rest(0)
-        place_rest(0)
         conv(0, 0, rows, True, False)
         wait_near(1)
         wait_far(1)
         place_near(1)
         place_far(1)
         wait_rest(1)
+        wait_rest(middle)
         place_rest(1)
-        conv(1, 0, rows, False, True)
+        conv(1, 0, rows, False, False)
+        place_near(2)
+        place_far(2)
+        wait_rest(5 - middle)
+        place_rest(2)
+        conv(2, 0, rows, False, True)
     else:
-        wait_edge(0)
+        for rel in range(4):
+            wait_rest(rel)
         for other in range(2):
-            wait_rest(other)
             wait_near(other)
             wait_far(other)
         place_rest(0)
@@ -475,7 +525,6 @@
     bf16 = jnp.bfloat16
     composed = total * CELLS <= width
     tap_width = total * CELLS if composed else width
-    groups = 2 if composed else 1
     any_space = pl.BlockSpec(memory_space=pltpu.HBM)
     vmem = pl.BlockSpec(memory_space=pltpu.VMEM)
     return pl.pallas_call(
@@ -499,7 +548,8 @@
             pltpu.VMEM((3, 3, width, width), bf16),
             pltpu.VMEM((3, 3, tap_width if composed else CELLS, width), bf16),
             pltpu.VMEM((9, 8, width), jnp.float32),
-            pltpu.VMEM((groups, (rows + 2) * row_slots, 3 * tap_width // groups), bf16),
+            pltpu.VMEM(((rows + 2) * row_slots, 3 * tap_width // (2 if composed else 1)), bf16),
+            pltpu.VMEM((2, rows * row_slots if composed else CELLS, 9 * tap_width // 4), bf16),
             pltpu.VMEM((rows * row_slots, width if composed else LANES), jnp.float32),
             pltpu.SemaphoreType.DMA,
             pltpu.SemaphoreType.DMA,
@@ -510,7 +560,7 @@
             pltpu.SemaphoreType.DMA,
             pltpu.SemaphoreType.DMA((2,)),
             pltpu.SemaphoreType.DMA((2,)),
-            pltpu.SemaphoreType.DMA((2,)),
+            pltpu.SemaphoreType.DMA((4,)),
             pltpu.SemaphoreType.DMA((2,)),
             pltpu.SemaphoreType.DMA((2,)),
         ],

time: 23.9 us -> 23 us (0.962)
  the two profiles are of different devices: /device:TPU:5 before, /device:TPU:0 now
where the time goes in v3:
time: 23 us; the launch traced here: 22.6 us
  Pallas kernels  21.7 us (94%)
  local copies, waits for them, and re-layouts  0.95 us (4%)
    pallas_call x1, Pallas kernels, per_device(): pl.pallas_call(functools.partial(kernel, dims), out_shape=jax.ShapeDtypeS...  21.7 us
    unnamed x1, local copies, waits for them, and re-layouts  0.95 us

profile of v3, /device:TPU:0, one launch (start us, length us, event | category | flops | bytes accessed | tf_op | source)
XLA Modules:
  0.0 22.6 jit_solution(3074947547264769246)
XLA Ops:
  0.0 21.7 %tiles.1 = bf16[5,90,1024]{2,1,0:T(8,128)(2,1)S(1)} custom-call(bf16[1,160,1440]{2,1,0:T(8,128)(2,1)} %raw_hbm.1, bf16[32,4,4,1024]{3,2,1,0:T(4,128)(2,1)} %ew_hbm.1, f32[1,1024]{1,0:T(1,128)} %bitcast.2, bf16[3,3,1024,1024]{3,2,1,0:T(8,128)(2,1)} %cw_hbm.1, f32[1,1024]{1,0:T(1,128)} %bitcast.3), custom_call_target="tpu_custom_call" | custom-call | tf_op jit(solution)/shard_map/tiles/pallas_call | solution.py:530
  21.7 0.9 %copy.7 = bf16[5,90,1024]{2,1,0:T(8,128)(2,1)} copy(bf16[5,90,1024]{2,1,0:T(8,128)(2,1)S(1)} %tiles.1) | data formatting | bytes 1843200
